TPU v7x, 256 devices: a whole 4x4x8 slice. The times are simulated.
256 devices in a mesh: freq: 8 (over x, core), rec: 32 (over z, y).
Axes of the slice: x: 4, y: 4, z: 8, core: 2. Of those that a mesh axis runs over, the one named last changes fastest.
Arguments:
- response_real: float32 [96, 1536, 1536], P('freq', 'rec'), may hold values from -0.109375 to 0.109375
- response_imaginary: float32 [96, 1536, 1536], P('freq', 'rec'), may hold values from -0.109375 to 0.109375
- focus: float32 [1536, 96, 128], P('rec', 'freq'), may hold values from -6 to 6
- initial: float32 [1536, 96, 128], P('rec', 'freq'), may hold values from -6 to 6
- onset: int32 [1536, 64], P('rec'), may hold values from 24 to 167
Outputs:
- focus_next: float32 [1536, 96, 128], P('rec', 'freq')
All inputs are finite; a program needn't handle non-finite values.
Results may differ from a plain program's by a relative error of at most 0.0003.
Values sent between devices are 32-bit elements; how exact they have to be, the bound alone decides.
No kernel may reach another device: no remote copies, remote signals or barrier semaphores. Data moves between devices by JAX's collectives and lax.ppermute only.
A program may use at most 128 MiB of HBM per device.

v0:
```python
import math
import jax
import jax.numpy as jnp
from jax import lax
from jax.sharding import Mesh
from jax.sharding import PartitionSpec as P

REC = ("rec_0", "rec_1")


def sum_by_axis(total, axes):
    for axis in axes:
        total = lax.psum_scatter(total, axis, scatter_dimension=0, tiled=True)
    return total


def tables(freqs):
    samples = 2 * freqs
    order = lax.iota(jnp.int32, freqs)
    sample = lax.iota(jnp.int32, samples)
    phase = order[:, None] * sample[None, :] % samples
    phases = 2.0 * math.pi / samples * phase.astype(jnp.float32)
    cosine = jnp.cos(phases)
    sine = jnp.sin(phases)
    factor = jnp.where(order == 0, 1.0, 2.0).astype(jnp.float32)[:, None] / samples
    inverse = jnp.stack([factor * cosine, -factor * sine])
    forward = jnp.stack([cosine, -sine])
    return (inverse, forward, sample)


def window(spectrum, onset):
    count, freqs, width = spectrum.shape
    half = width // 2
    inverse, forward, sample = tables(freqs)
    split = spectrum.reshape(count, freqs, 2, half)
    traces = jnp.einsum("nkcp,ckt->ntp", split, inverse, precision=lax.Precision.HIGHEST)
    keep = sample[None, :, None] < onset[:, None, :]
    clipped = jnp.where(keep, traces, 0.0)
    back = jnp.einsum("ntp,ckt->nkcp", clipped, forward, precision=lax.Precision.HIGHEST)
    return back.reshape(count, freqs, width)


def adjoint_terms(real_part, imag_part, values):
    half = values.shape[2] // 2
    first = jnp.einsum("frs,rfq->sfq", real_part, values, precision=lax.Precision.HIGHEST)
    second = jnp.einsum("frs,rfq->sfq", imag_part, values, precision=lax.Precision.HIGHEST)
    return jnp.concatenate(
        [first[..., :half] + second[..., half:], first[..., half:] - second[..., :half]], axis=2
    )


def forward_terms(real_part, imag_part, values):
    half = values.shape[2] // 2
    first = jnp.einsum("frs,sfq->rfq", real_part, values, precision=lax.Precision.HIGHEST)
    second = jnp.einsum("frs,sfq->rfq", imag_part, values, precision=lax.Precision.HIGHEST)
    return jnp.concatenate(
        [first[..., :half] - second[..., half:], first[..., half:] + second[..., :half]], axis=2
    )


def onset_rows(onset):
    owned = onset.shape[0] // lax.axis_size("freq")
    return lax.dynamic_slice_in_dim(onset, lax.axis_index("freq") * owned, owned, 0)


def iterate(response_real, response_imaginary, values, onset):
    local_onset = onset_rows(onset)
    real_cols = response_real
    imag_cols = response_imaginary
    partial_sum = sum_by_axis(adjoint_terms(real_cols, imag_cols, values), REC)
    turned = lax.all_to_all(partial_sum, "freq", split_axis=0, concat_axis=1, tiled=True)
    windowed = window(turned, local_onset)
    returned = lax.all_to_all(windowed, "freq", split_axis=1, concat_axis=0, tiled=True)
    real_cols = response_real
    imag_cols = response_imaginary
    forward = forward_terms(real_cols, imag_cols, lax.all_gather(returned, REC, axis=0, tiled=True))
    receiver_side = lax.all_to_all(forward, "freq", split_axis=0, concat_axis=1, tiled=True)
    clipped = window(receiver_side, local_onset)
    return lax.all_to_all(clipped, "freq", split_axis=1, concat_axis=0, tiled=True)


def on_device(response_real, response_imaginary, focus, initial, onset):
    real_used, imag_used = (response_real, response_imaginary)
    update = iterate(real_used, imag_used, focus, onset)
    return initial - update


def solution(mesh):
    finer = Mesh(mesh.devices.reshape(mesh.shape["freq"], 8, 4), ("freq", "rec_0", "rec_1"))
    in_specs = (
        P("freq", REC, None),
        P("freq", REC, None),
        P(REC, "freq", None),
        P(REC, "freq", None),
        P(REC, None),
    )
    out_specs = P(REC, "freq", None)
    return jax.shard_map(
        on_device, mesh=finer, in_specs=in_specs, out_specs=out_specs, check_vma=False
    )
```

profile of v0, /device:TPU:1, one launch (start us, length us, event | category | flops | bytes accessed | tf_op | source)
XLA Modules:
  0.0 388.9 jit_solution(16803704345804091583)
XLA Ops:
  6.5 2.0 copy-done
  8.5 8.9 %convolution_bitcast_fusion = f32[1536,12,128]{0,2,1:T(8,128)S(1)} fusion(f32[48,12,128]{2,0,1:T(8,128)} %param.7, f32[12,48,1536]{2,1,0:T(8,128)S(1)} %copy-done), kind=kOutput, calls=%fused_computation.1 | convolution fusion | flops 1358954496 | bytes 13271040 | tf_op jit(solution)/shard_map/frs,rfq->sfq/dot_general | solution.py:46
  17.5 8.0 %convolution_bitcast_fusion.1 = f32[1536,12,128]{0,2,1:T(8,128)S(1)} fusion(f32[48,12,128]{2,0,1:T(8,128)S(1)} %copy-done.4, f32[12,48,1536]{2,1,0:T(8,128)S(1)} %copy-done.2), kind=kOutput, calls=%fused_computation.2 | convolution fusion | flops 1358954496 | bytes 13271040 | tf_op jit(solution)/shard_map/frs,rfq->sfq/dot_general | solution.py:45
  25.5 3.5 slice_add_fusion
  29.0 7.3 %pad_maximum_fusion = f32[1536,12,128]{0,2,1:T(8,128)} fusion(f32[1536,12,64]{0,2,1:T(8,128)} %get-tuple-element.6, f32[1536,12,64]{0,2,1:T(8,128)S(1)} %get-tuple-element.5), kind=kLoop, calls=%fused_computation | loop fusion | flops 2359296 | bytes 18874368 | tf_op jit(solution)/shard_map/concatenate | solution.py:47
  36.3 9.6 %copy.44 = f32[1536,1536]{1,0:T(8,128)} copy(f32[1536,1536]{0,1:T(8,128)} %bitcast.81) | data formatting | bytes 18874368
  46.0 108.7 %reduce-scatter.7.cloned.1.call-done = f32[192,1536]{1,0:T(8,128)} async-done(((f32[1536,1536]{1,0:T(8,128)}), f32[192,1536]{1,0:T(8,128)}) %reduce-scatter.7.cloned.1.call-update) | async-done | bytes 1179664
  154.6 2.9 copy.45
  157.5 3.4 copy.15
  161.6 1.1 fusion.11
  162.8 24.4 %reduce-scatter.5.cloned.1.call-done = f32[48,12,128]{2,1,0:T(8,128)} async-done(((f32[192,12,128]{2,1,0:T(8,128)}), f32[48,12,128]{2,1,0:T(8,128)}) %reduce-scatter.5.cloned.1.call-update) | async-done | bytes 294928 | tf_op jit(solution)/shard_map/reduce_scatter | solution.py:13
  187.2 5.7 %all-to-all-start = ((f32[48,12,128]{2,1,0:T(8,128)}), f32[48,12,128]{2,1,0:T(8,128)}, u32[]{:S(2)}, u32[]{:S(2)}) async-start(f32[48,12,128]{2,1,0:T(8,128)} %reduce-scatter.5.cloned.1.call-done), calls=%async_computation.1 | async-start | bytes 786432 | tf_op jit(solution)/shard_map/all_to_all | solution.py:71
  192.9 1.1 fusion.12
  194.0 6.7 %all-to-all-done = f32[48,12,128]{2,1,0:T(8,128)} async-done(((f32[48,12,128]{2,1,0:T(8,128)}), f32[48,12,128]{2,1,0:T(8,128)}, u32[]{:S(2)}, u32[]{:S(2)}) %all-to-all-start) | async-done | bytes 294944 | tf_op jit(solution)/shard_map/all_to_all | solution.py:71
  200.7 1.8 copy.17
  202.5 2.2 reshape.140
  204.6 2.3 fusion.1
  206.9 1.4 convolution_bitcast_fusion.4
  209.2 1.9 copy.20
  211.1 12.6 %all_to_all.66 = f32[6,96,128]{2,0,1:T(8,128)S(1)} all-to-all(f32[6,96,128]{2,0,1:T(8,128)} %copy.20), channel_id=1, replica_groups=mesh['freq'=8,'rec_0'=8,'rec_1'=4] {'freq'}, dimensions={1} | all-to-all | bytes 589824 | tf_op jit(solution)/shard_map/all_to_all | solution.py:73
  224.5 1.7 all_to_all.54
  226.3 100.8 %all-gather.2.cloned.1.call-done = f32[1536,12,128]{2,0,1:T(8,128)} async-done(((f32[48,12,128]{2,0,1:T(8,128)}), f32[1536,12,128]{2,0,1:T(8,128)}) %all-gather.2.cloned.1.call-update) | async-done | bytes 9437200 | tf_op jit(solution)/shard_map/all_gather | solution.py:76
  327.1 9.3 %convolution_bitcast_fusion.6 = f32[48,12,128]{2,0,1:T(8,128)S(1)} fusion(f32[1536,12,128]{2,0,1:T(8,128)} %all-gather.2.cloned.1.call-done, f32[12,48,1536]{2,1,0:T(8,128)S(1)} %copy-done), kind=kOutput, calls=%fused_computation.9 | convolution fusion | flops 1358954496 | bytes 13271040 | tf_op jit(solution)/shard_map/frs,sfq->rfq/dot_general | solution.py:55
  336.4 6.0 %convolution_bitcast_fusion.7 = f32[48,12,128]{2,0,1:T(8,128)S(1)} fusion(f32[1536,12,128]{2,0,1:T(8,128)S(1)} %copy-done.1, f32[12,48,1536]{2,1,0:T(8,128)S(1)} %copy-done.3), kind=kOutput, calls=%fused_computation.10 | convolution fusion | flops 1358954496 | bytes 13271040 | tf_op jit(solution)/shard_map/frs,sfq->rfq/dot_general | solution.py:54
  342.9 13.5 %all_to_all.67 = f32[48,12,128]{2,1,0:T(8,128)S(1)} all-to-all(f32[48,12,128]{2,1,0:T(8,128)S(1)} %copy.23), channel_id=1, replica_groups=mesh['freq'=8,'rec_0'=8,'rec_1'=4] {'freq'}, dimensions={0} | all-to-all | bytes 589824 | tf_op jit(solution)/shard_map/all_to_all | solution.py:77
  357.2 2.2 reshape.142
  359.3 2.3 fusion.3
  361.6 1.4 convolution_bitcast_fusion.2
  363.9 1.9 copy.28
  365.8 12.3 %all_to_all.68 = f32[6,96,128]{2,0,1:T(8,128)S(1)} all-to-all(f32[6,96,128]{2,0,1:T(8,128)} %copy.28), channel_id=1, replica_groups=mesh['freq'=8,'rec_0'=8,'rec_1'=4] {'freq'}, dimensions={1} | all-to-all | bytes 589824 | tf_op jit(solution)/shard_map/all_to_all | solution.py:79
  378.9 1.7 all_to_all.61
  380.6 1.8 sub.11
  (26 shorter events, 5.2 us)
Async XLA Ops:
  6.5 2.0 copy-start
  6.5 148.1 %reduce-scatter.7.cloned.1.call-start = ((), (), s32[]{:S(2)}) async-start(), calls=%async_computation.8 | async-start | bytes 10616832
  8.5 8.9 %copy-start.2 = (f32[12,48,1536]{2,1,0:T(8,128)S(1)}, f32[12,48,1536]{2,1,0:T(8,128)}, u32[]{:S(2)}) copy-start(f32[12,48,1536]{2,1,0:T(8,128)} %param.5) | copy-start | bytes 10616836
  8.5 9.0 %copy-start.4 = (f32[48,12,128]{2,0,1:T(8,128)S(1)}, f32[48,12,128]{2,0,1:T(8,128)}, u32[]{:S(2)}) copy-start(f32[48,12,128]{2,0,1:T(8,128)} %param.7) | copy-start | bytes 884740
  45.9 141.2 %reduce-scatter.5.cloned.1.call-start = ((), (), s32[]{:S(2)}) async-start(), calls=%async_computation.6 | async-start | bytes 1966080 | tf_op jit(solution)/shard_map/reduce_scatter | solution.py:13
  187.2 13.5 %all-to-all-start = ((f32[48,12,128]{2,1,0:T(8,128)}), f32[48,12,128]{2,1,0:T(8,128)}, u32[]{:S(2)}, u32[]{:S(2)}) async-start(f32[48,12,128]{2,1,0:T(8,128)} %reduce-scatter.5.cloned.1.call-done), calls=%async_computation.1 | async-start | bytes 786432 | tf_op jit(solution)/shard_map/all_to_all | solution.py:71
  192.9 134.2 %all-gather.2.cloned.1.call-start = ((), (), s32[]{:S(2)}) async-start(), calls=%async_computation.7 | async-start | bytes 9732096 | tf_op jit(solution)/shard_map/all_gather | solution.py:76
  327.1 9.3 %copy-start.1 = (f32[1536,12,128]{2,0,1:T(8,128)S(1)}, f32[1536,12,128]{2,0,1:T(8,128)}, u32[]{:S(2)}) copy-start(f32[1536,12,128]{2,0,1:T(8,128)} %all-gather.2.cloned.1.call-done) | copy-start | bytes 28311556
  327.1 9.3 %copy-start.3 = (f32[12,48,1536]{2,1,0:T(8,128)S(1)}, f32[12,48,1536]{2,1,0:T(8,128)}, u32[]{:S(2)}) copy-start(f32[12,48,1536]{2,1,0:T(8,128)} %param.5) | copy-start | bytes 10616836
Sparse Core Ops, SparseCore 0:
  46.0 108.5 reduce-scatter.6
  161.0 26.0 reduce-scatter.4
  226.4 100.6 all-gather.1
where the time goes:
time: 390 us; the launch traced here: 389 us
  waiting for transfers between devices  241 us (62%)
  matrix products  39.7 us (10%)
  blocking collectives  38.4 us (10%)
  local copies, waits for them, and re-layouts  36 us (9%)
  other arithmetic  15.2 us (4%)
  between operations  13.2 us (3%)
  starting transfers between devices  5.78 us (1%)
    unnamed x4, waiting for transfers between devices  109 us
    all_gather x1, waiting for transfers between devices, iterate(): lax.all_gather(returned, REC, axis=0, tiled=True)  101 us
    reduce_scatter x1, waiting for transfers between devices, sum_by_axis(): total = lax.psum_scatter(total, axis, scatter_dimension=0, tiled=True)  24.4 us
    unnamed x12, local copies, waits for them, and re-layouts  14.5 us
    all_to_all x1, blocking collectives, iterate(): lax.all_to_all(forward, 'freq', split_axis=0, concat_axis=1, tiled=True)  13.5 us
    all_to_all x1, blocking collectives, iterate(): lax.all_to_all(windowed, 'freq', split_axis=1, concat_axis=0, tiled=True)  12.6 us
    all_to_all x1, blocking collectives, iterate(): lax.all_to_all(clipped, 'freq', split_axis=1, concat_axis=0, tiled=True)  12.3 us
    dot_general x1, matrix products, forward_terms(): jnp.einsum('frs,sfq->rfq', imag_part, values, precision=lax.Precision.HIG...  9.26 us
  transfers between devices with their start and end apart: 4, of which 4 were waited for; matrix products, arithmetic and copies ran while one was open for 1% of the time, Pallas kernels for 0%

commit v1 on v0

--- a/solution.py
+++ b/solution.py
@@ -73,7 +73,19 @@
     returned = lax.all_to_all(windowed, "freq", split_axis=1, concat_axis=0, tiled=True)
     real_cols = response_real
     imag_cols = response_imaginary
-    forward = forward_terms(real_cols, imag_cols, lax.all_gather(returned, REC, axis=0, tiled=True))
+    forward = forward_terms(
+        real_cols,
+        imag_cols,
+        jnp.concatenate(
+            lax.all_to_all(
+                jnp.stack([returned for _ in range(lax.axis_size(REC))], axis=0),
+                REC,
+                split_axis=0,
+                concat_axis=0,
+            ),
+            axis=0,
+        ),
+    )
     receiver_side = lax.all_to_all(forward, "freq", split_axis=0, concat_axis=1, tiled=True)
     clipped = window(receiver_side, local_onset)
     return lax.all_to_all(clipped, "freq", split_axis=1, concat_axis=0, tiled=True)

time: 390 us -> 516 us (1.32); the launches traced: 389 us -> 506 us
  blocking collectives: 38.4 us -> 252 us
  waiting for transfers between devices: 241 us -> 140 us
  local copies, waits for them, and re-layouts: 36 us -> 42.7 us
    all_to_all x0 -> x1, blocking collectives: none -> 214 us  [iterate(): lax.all_to_all(jnp.stack([returned for _ in range(lax.axis_size(REC))], a...]
    all_gather x1 -> x0, waiting for transfers between devices: 101 us -> none  [iterate(): lax.all_gather(returned, REC, axis=0, tiled=True)]
    unnamed x4 -> x3, waiting for transfers between devices: 109 us -> 109 us
    unnamed x12 -> x10, local copies, waits for them, and re-layouts: 14.5 us -> 14.5 us
  transfers between devices with their start and end apart: 4 -> 3, of which waited for: 4 -> 3; matrix products, arithmetic and copies ran while one was open for 1% -> 1% of each run, Pallas kernels for 0% -> 0%
where the time goes in v1:
time: 516 us; the launch traced here: 506 us
  blocking collectives  252 us (49%)
  waiting for transfers between devices  140 us (27%)
  local copies, waits for them, and re-layouts  42.7 us (8%)
  matrix products  37 us (7%)
  other arithmetic  15.2 us (3%)
  between operations  13.8 us (3%)
  starting transfers between devices  5.77 us (1%)
    all_to_all x1, blocking collectives, iterate(): lax.all_to_all(jnp.stack([returned for _ in range(lax.axis_size(REC))], a...  214 us
    unnamed x3, waiting for transfers between devices  109 us
    reduce_scatter x1, waiting for transfers between devices, sum_by_axis(): total = lax.psum_scatter(total, axis, scatter_dimension=0, tiled=True)  24.4 us
    unnamed x10, local copies, waits for them, and re-layouts  14.5 us
    all_to_all x1, blocking collectives, iterate(): lax.all_to_all(forward, 'freq', split_axis=0, concat_axis=1, tiled=True)  13.3 us
    all_to_all x1, blocking collectives, iterate(): lax.all_to_all(windowed, 'freq', split_axis=1, concat_axis=0, tiled=True)  12.6 us
    all_to_all x1, blocking collectives, iterate(): lax.all_to_all(clipped, 'freq', split_axis=1, concat_axis=0, tiled=True)  12.3 us
  transfers between devices with their start and end apart: 3, of which 3 were waited for; matrix products, arithmetic and copies ran while one was open for 1% of the time, Pallas kernels for 0%

profile of v1, /device:TPU:1, one launch (start us, length us, event | category | flops | bytes accessed | tf_op | source)
XLA Modules:
  0.0 506.3 jit_solution(5293982630117297760)
XLA Ops:
  6.5 2.0 copy-done
  8.5 8.9 %convolution_bitcast_fusion = f32[1536,12,128]{0,2,1:T(8,128)S(1)} fusion(f32[48,12,128]{2,0,1:T(8,128)} %param.7, f32[12,48,1536]{2,1,0:T(8,128)S(1)} %copy-done), kind=kOutput, calls=%fused_computation.1 | convolution fusion | flops 1358954496 | bytes 13271040 | tf_op jit(solution)/shard_map/frs,rfq->sfq/dot_general | solution.py:46
  17.5 8.3 %convolution_bitcast_fusion.1 = f32[1536,12,128]{0,2,1:T(8,128)S(1)} fusion(f32[48,12,128]{2,0,1:T(8,128)S(1)} %copy-done.3, f32[12,48,1536]{2,1,0:T(8,128)S(1)} %copy-done.1), kind=kOutput, calls=%fused_computation.2 | convolution fusion | flops 1358954496 | bytes 13271040 | tf_op jit(solution)/shard_map/frs,rfq->sfq/dot_general | solution.py:45
  25.8 3.5 slice_add_fusion
  29.3 7.3 %pad_maximum_fusion = f32[1536,12,128]{0,2,1:T(8,128)} fusion(f32[1536,12,64]{0,2,1:T(8,128)} %get-tuple-element.6, f32[1536,12,64]{0,2,1:T(8,128)S(1)} %get-tuple-element.5), kind=kLoop, calls=%fused_computation | loop fusion | flops 2359296 | bytes 18874368 | tf_op jit(solution)/shard_map/concatenate | solution.py:47
  36.6 9.6 %copy.45 = f32[1536,1536]{1,0:T(8,128)} copy(f32[1536,1536]{0,1:T(8,128)} %bitcast.84) | data formatting | bytes 18874368
  46.2 108.7 %reduce-scatter.7.cloned.1.call-done = f32[192,1536]{1,0:T(8,128)} async-done(((f32[1536,1536]{1,0:T(8,128)}), f32[192,1536]{1,0:T(8,128)}) %reduce-scatter.7.cloned.1.call-update) | async-done | bytes 1179664
  154.9 2.9 copy.46
  157.8 3.4 copy.15
  163.0 24.4 %reduce-scatter.5.cloned.1.call-done = f32[48,12,128]{2,1,0:T(8,128)} async-done(((f32[192,12,128]{2,1,0:T(8,128)}), f32[48,12,128]{2,1,0:T(8,128)}) %reduce-scatter.5.cloned.1.call-update) | async-done | bytes 294928 | tf_op jit(solution)/shard_map/reduce_scatter | solution.py:13
  187.4 5.7 %all-to-all-start = ((f32[48,12,128]{2,1,0:T(8,128)}), f32[48,12,128]{2,1,0:T(8,128)}, u32[]{:S(2)}, u32[]{:S(2)}) async-start(f32[48,12,128]{2,1,0:T(8,128)} %reduce-scatter.5.cloned.1.call-done), calls=%async_computation.1 | async-start | bytes 786432 | tf_op jit(solution)/shard_map/all_to_all | solution.py:71
  194.3 6.7 %all-to-all-done = f32[48,12,128]{2,1,0:T(8,128)} async-done(((f32[48,12,128]{2,1,0:T(8,128)}), f32[48,12,128]{2,1,0:T(8,128)}, u32[]{:S(2)}, u32[]{:S(2)}) %all-to-all-start) | async-done | bytes 294944 | tf_op jit(solution)/shard_map/all_to_all | solution.py:71
  200.9 1.8 copy.17
  202.7 2.2 reshape.146
  204.9 2.3 fusion.1
  207.2 1.4 convolution_bitcast_fusion.4
  209.4 1.9 copy.20
  211.4 12.6 %all_to_all.68 = f32[6,96,128]{2,0,1:T(8,128)S(1)} all-to-all(f32[6,96,128]{2,0,1:T(8,128)} %copy.20), channel_id=1, replica_groups=mesh['freq'=8,'rec_0'=8,'rec_1'=4] {'freq'}, dimensions={1} | all-to-all | bytes 589824 | tf_op jit(solution)/shard_map/all_to_all | solution.py:73
  224.8 1.7 stack.10
  226.5 2.0 stack.11
  228.5 213.9 %all_to_all.69 = f32[32,48,12,128]{3,1,2,0:T(8,128)} all-to-all(f32[32,48,12,128]{3,1,2,0:T(8,128)S(1)} %stack.11), channel_id=1, replica_groups=mesh['freq'=8,'rec_0'=8,'rec_1'=4] {'rec_0','rec_1'}, dimensions={0} | all-to-all | bytes 18874368 | tf_op jit(solution)/shard_map/all_to_all | solution.py:80
  442.4 4.6 copy.23
  447.1 6.0 %convolution_bitcast_fusion.6 = f32[48,12,128]{2,0,1:T(8,128)S(1)} fusion(f32[1536,12,128]{2,0,1:T(8,128)S(1)} %bitcast.82, f32[12,48,1536]{2,1,0:T(8,128)S(1)} %copy-done), kind=kOutput, calls=%fused_computation.9 | convolution fusion | flops 1358954496 | bytes 13271040 | tf_op jit(solution)/shard_map/frs,sfq->rfq/dot_general | solution.py:55
  453.1 6.3 %convolution_bitcast_fusion.7 = f32[48,12,128]{2,0,1:T(8,128)S(1)} fusion(f32[1536,12,128]{2,0,1:T(8,128)S(1)} %bitcast.83, f32[12,48,1536]{2,1,0:T(8,128)S(1)} %copy-done.2), kind=kOutput, calls=%fused_computation.10 | convolution fusion | flops 1358954496 | bytes 13271040 | tf_op jit(solution)/shard_map/frs,sfq->rfq/dot_general | solution.py:54
  459.9 13.3 %all_to_all.70 = f32[48,12,128]{2,1,0:T(8,128)S(1)} all-to-all(f32[48,12,128]{2,1,0:T(8,128)S(1)} %copy.24), channel_id=1, replica_groups=mesh['freq'=8,'rec_0'=8,'rec_1'=4] {'freq'}, dimensions={0} | all-to-all | bytes 589824 | tf_op jit(solution)/shard_map/all_to_all | solution.py:89
  474.0 2.2 reshape.149
  476.2 2.3 fusion.3
  478.5 1.5 convolution_bitcast_fusion.2
  480.7 1.9 copy.29
  482.7 12.3 %all_to_all.71 = f32[6,96,128]{2,0,1:T(8,128)S(1)} all-to-all(f32[6,96,128]{2,0,1:T(8,128)} %copy.29), channel_id=1, replica_groups=mesh['freq'=8,'rec_0'=8,'rec_1'=4] {'freq'}, dimensions={1} | all-to-all | bytes 589824 | tf_op jit(solution)/shard_map/all_to_all | solution.py:91
  495.7 1.7 all_to_all.62
  497.4 1.8 sub.11
  (24 shorter events, 7.4 us)
Async XLA Ops:
  6.5 2.0 copy-start
  6.5 148.3 %reduce-scatter.7.cloned.1.call-start = ((), (), s32[]{:S(2)}) async-start(), calls=%async_computation.8 | async-start | bytes 10616832
  8.5 8.9 %copy-start.1 = (f32[12,48,1536]{2,1,0:T(8,128)S(1)}, f32[12,48,1536]{2,1,0:T(8,128)}, u32[]{:S(2)}) copy-start(f32[12,48,1536]{2,1,0:T(8,128)} %param.5) | copy-start | bytes 10616836
  8.5 9.0 %copy-start.3 = (f32[48,12,128]{2,0,1:T(8,128)S(1)}, f32[48,12,128]{2,0,1:T(8,128)}, u32[]{:S(2)}) copy-start(f32[48,12,128]{2,0,1:T(8,128)} %param.7) | copy-start | bytes 884740
  46.2 141.2 %reduce-scatter.5.cloned.1.call-start = ((), (), s32[]{:S(2)}) async-start(), calls=%async_computation.7 | async-start | bytes 1966080 | tf_op jit(solution)/shard_map/reduce_scatter | solution.py:13
  187.4 13.5 %all-to-all-start = ((f32[48,12,128]{2,1,0:T(8,128)}), f32[48,12,128]{2,1,0:T(8,128)}, u32[]{:S(2)}, u32[]{:S(2)}) async-start(f32[48,12,128]{2,1,0:T(8,128)} %reduce-scatter.5.cloned.1.call-done), calls=%async_computation.1 | async-start | bytes 786432 | tf_op jit(solution)/shard_map/all_to_all | solution.py:71
  447.1 6.0 %copy-start.2 = (f32[12,48,1536]{2,1,0:T(8,128)S(1)}, f32[12,48,1536]{2,1,0:T(8,128)}, u32[]{:S(2)}) copy-start(f32[12,48,1536]{2,1,0:T(8,128)} %param.5) | copy-start | bytes 10616836
Sparse Core Ops, SparseCore 0:
  46.3 108.5 reduce-scatter.6
  161.3 26.0 reduce-scatter.4
